TPU v7x, 8 devices: a whole 2x2x1 slice. The times are simulated.
8 devices in a mesh: data: 8 (over z, y, x, core).
Axes of the slice: x: 2, y: 2, z: 1, core: 2. Of those that a mesh axis runs over, the one named last changes fastest.
Arguments:
- view_one: bfloat16 [1024, 256], P('data')
- view_two: bfloat16 [1024, 256], P('data')
- protos: bfloat16 [16384, 256], replicated
- valid_mask: int32 [1024], P('data')
Outputs:
- output 1: float32 [1024, 16384], P('data')
- output 2: float32 [1024, 16384], P('data')
- output 3: float32 [], replicated
- output 4: float32 [1024, 256], P('data')
- output 5: float32 [1024, 256], P('data')
- output 6: float32 [16384, 256], replicated
All inputs are finite; a program needn't handle non-finite values.
Results may differ from a plain program's by a relative error of at most 0.001.
Values are sent between devices in bfloat16 or wider.
A program may use at most 1 GiB of HBM per device.

v0:
```python
import functools

import jax
import jax.numpy as jnp
from jax import lax
from jax.experimental import pallas as pl
from jax.experimental.pallas import tpu as pltpu
from jax.sharding import PartitionSpec as P

SOFT_TEMP = 0.1
LOG2E = 1.4426950408889634
C_EXP = LOG2E / SOFT_TEMP
MESH = pl.DeviceIdType.MESH
NDEV = 8
ROWS = 128
NS = NDEV * ROWS
DIM = 256
KALL = 16384
KLOC = KALL // NDEV
GRP = 128
CH = 256
TK = 4096
SUB = 512
CK = 1024
OS = 256

PCH = 1024
NPC = KALL // PCH
NBUF = 4
SPLIT = (10, 12, 14, 16)

VM1 = 53
VM2 = 45
NT_DIMS = (((1,), (1,)), ((), ()))


def dot_nt(x, y):
    return lax.dot_general(x, y, NT_DIMS, preferred_element_type=jnp.float32)


def dot_nn(x, y):
    return jnp.dot(x, y, preferred_element_type=jnp.float32)


def sink_kernel(z1_hbm, z2_hbm, m_hbm, c_hbm,
                w_ref, vecs_ref, own_ref, b_out, stat_ref, p0_out, c0_out, p_hbm,
                z_all, m_all, cs, ps, zcs, s_ref, e_ref, bcol,
                ar1, ar1b, ar2, ar2b, ar3, ar3b, b_all, zz, cbuf, pbuf,
                c_sem, in_sem, m_send, m_recv, z_send, z_recv, f_send, f_recv,
                ar_send, ar_recv, b_send, b_recv, cb_sem, pb_sem):
    me = lax.axis_index("data")
    chip, core = me // 2, me % 2
    partner = 2 * chip + (1 - core)
    peers = [lax.rem(me + o, NDEV) for o in range(1, NDEV)]
    same = [2 * lax.rem(chip + d, 4) + core for d in range(1, 4)]

    barrier = pltpu.get_barrier_semaphore()
    for peer in peers:
        pl.semaphore_signal(barrier, inc=1, device_id=(peer,), device_id_type=MESH)

    loads = [pltpu.make_async_copy(src, dst, in_sem.at[i]) for i, (src, dst) in enumerate((
        (z1_hbm, z_all.at[0, me]), (z2_hbm, z_all.at[1, me]), (m_hbm, m_all.at[me]),
        (z1_hbm, zz.at[pl.ds(0, ROWS)]), (z2_hbm, zz.at[pl.ds(ROWS, ROWS)])))]
    for cp in loads:
        cp.start()

    def c_load(j):
        dst = c0_out.at[pl.ds(j * PCH, PCH), :] if j < TK // PCH else cbuf.at[j % NBUF]
        return pltpu.make_async_copy(c_hbm.at[pl.ds(j * PCH, PCH), :], dst, cb_sem.at[j % NBUF])

    def p_store(j):
        return pltpu.make_async_copy(
            pbuf.at[j % NBUF], p_hbm.at[:, pl.ds(j * PCH - TK, PCH)], pb_sem.at[j % NBUF])

    for j in range(NBUF):
        c_load(j).start()
    cslice = pltpu.make_async_copy(c_hbm.at[pl.ds(me * KLOC, KLOC), :], cs, c_sem)
    cslice.start()

    def own_scores(lo, hi):
        for j in range(lo, hi):
            c_load(j).wait()
            if j - NBUF >= TK // PCH:
                p_store(j - NBUF).wait()
            for t in range(PCH // 256):
                cols = slice(t * 256, (t + 1) * 256)
                rows = slice(j * PCH + t * 256, j * PCH + (t + 1) * 256)
                sc = dot_nt(zz[...], c0_out[rows, :] if j < TK // PCH else cbuf[j % NBUF, cols, :])
                if j < TK // PCH:
                    p0_out[:, j * PCH + t * 256:j * PCH + (t + 1) * 256] = jnp.exp2(sc * C_EXP)
                else:
                    pbuf[j % NBUF, :, cols] = jnp.exp2(sc * C_EXP)
            if j >= TK // PCH:
                p_store(j).start()
            if j + NBUF < NPC:
                c_load(j + NBUF).start()

    for cp in loads:
        cp.wait()
    pl.semaphore_wait(barrier, NDEV - 1)

    m_copies = []
    for o, peer in enumerate(peers):
        cp = pltpu.make_async_remote_copy(
            src_ref=m_all.at[me], dst_ref=m_all.at[me], send_sem=m_send.at[o],
            recv_sem=m_recv.at[o], device_id=(peer,), device_id_type=MESH)
        cp.start()
        m_copies.append(cp)
    z_copies = []
    for v in range(2):
        row = []
        for d, peer in enumerate(same + [partner]):
            cp = pltpu.make_async_remote_copy(
                src_ref=z_all.at[v, me], dst_ref=z_all.at[v, me], send_sem=z_send.at[v, d],
                recv_sem=z_recv.at[v, d], device_id=(peer,), device_id_type=MESH)
            cp.start()
            row.append(cp)
        z_copies.append(row)

    own_scores(0, SPLIT[0])
    for cp in m_copies:
        cp.wait_recv()
    mf = [jnp.broadcast_to(m_all[d].astype(jnp.float32), (8, ROWS)) for d in range(NDEV)]

    tri = (lax.broadcasted_iota(jnp.int32, (ROWS, ROWS), 0)
           < lax.broadcasted_iota(jnp.int32, (ROWS, ROWS), 1)).astype(jnp.bfloat16)
    base = jnp.zeros((8, 1), jnp.float32)
    pos_list = []
    for d in range(NDEV):
        md = mf[d]
        pre = dot_nn(md.astype(jnp.bfloat16), tri) + base
        pos_list.append(jnp.where(md > 0, pre, -1.0))
        base = base + jnp.sum(md, axis=1, keepdims=True)
    pos = jnp.concatenate(pos_list, axis=1)
    count = base
    mask = (lax.broadcasted_iota(jnp.int32, (8, NS), 1).astype(jnp.float32) < count)
    maskf = mask.astype(jnp.float32)
    for t in range(NS // 128):
        lo_col = t // 2 * 256
        idx = (lax.broadcasted_iota(jnp.int32, (128, NS - lo_col), 0) + t * 128).astype(jnp.float32)
        ps[t * 128:(t + 1) * 128, lo_col:] = (
            jnp.broadcast_to(pos[0:1, lo_col:], (128, NS - lo_col)) == idx).astype(jnp.bfloat16)

    def forward(v):
        out = []
        for d in range(3):
            z_copies[v][d].wait_recv()
            frm = 2 * lax.rem(chip + 3 - d, 4) + core
            cp = pltpu.make_async_remote_copy(
                src_ref=z_all.at[v, frm], dst_ref=z_all.at[v, frm], send_sem=f_send.at[v, d],
                recv_sem=f_recv.at[v, d], device_id=(partner,), device_id_type=MESH)
            cp.start()
            out.append(cp)
        return out

    def compact(v, fw):
        z_copies[v][3].wait_recv()
        for cp in fw:
            cp.wait_recv()
        zv = z_all[v].reshape(NS, DIM)
        for t in range(NS // 256):
            rows = slice(t * 256, (t + 1) * 256)
            zc = dot_nn(ps[rows, t * 256:], zv[t * 256:]).astype(jnp.bfloat16)
            zcs[v, rows, :] = zc
            w_ref[2 * t, v * ROWS:(v + 1) * ROWS, :] = zc[:ROWS]
            w_ref[2 * t + 1, v * ROWS:(v + 1) * ROWS, :] = zc[ROWS:]

    def exchange(idx, buf):
        copies = []
        for o, peer in enumerate(peers):
            cp = pltpu.make_async_remote_copy(
                src_ref=buf.at[me], dst_ref=buf.at[me], send_sem=ar_send.at[idx, o],
                recv_sem=ar_recv.at[idx, o], device_id=(peer,), device_id_type=MESH)
            cp.start()
            copies.append(cp)
        return copies

    def total(buf, copies):
        for cp in copies:
            cp.wait_recv()
        acc = buf[0]
        for d in range(1, NDEV):
            acc = acc + buf[d]
        return acc

    def rsum(x):
        return jnp.sum(x, axis=0, keepdims=True)

    m1 = maskf[0:1]

    def recip(r):
        return jnp.where(m1 > 0, 1.0 / jnp.where(m1 > 0, r, 1.0), 0.0)

    zero = jnp.zeros((8, NS), jnp.float32)

    def first_pass(v, lo, hi, carry):
        racc, lacc = carry

        def rows_part(i, racc):
            for g in range(CH // 8):
                rows = slice(i * CH + g * 8, i * CH + g * 8 + 8)
                b = jnp.concatenate([bcol[v, rows, :]] * (NS // 128), axis=1)
                racc = racc + e_ref[v, rows, :] * b
            return racc

        for i in range(lo, hi):
            off = i * CH
            s_ref[v, off:off + CH, :] = dot_nt(cs[off:off + CH, :], zcs[v])
            for g in range(CH // 8):
                rows = slice(off + g * 8, off + g * 8 + 8)
                p = jnp.exp2(s_ref[v, rows, :] * C_EXP)
                lacc = lacc + p
                e = p * p * maskf
                e_ref[v, rows, :] = e
                bcol[v, rows, :] = jnp.broadcast_to(1.0 / jnp.sum(e, axis=1, keepdims=True), (8, 128))
            if i > lo:
                racc = rows_part(i - 1, racc)
        return rows_part(hi - 1, racc), lacc

    def sweep(v, a, last):
        a8 = jnp.broadcast_to(a, (8, NS))

        def body(i, carry):
            carry = list(carry)
            off = pl.multiple_of(i * (GRP * 8), GRP * 8)
            for g in range(GRP):
                rows = pl.ds(off + g * 8, 8)
                e = e_ref[v, rows, :]
                b = 1.0 / jnp.sum(e * a8, axis=1, keepdims=True)
                eb = e * b
                carry[0] = carry[0] + eb
                if last:
                    bcol[v, rows, :] = jnp.broadcast_to(b, (8, 128))
                    carry[1] = carry[1] + eb * s_ref[1 - v, rows, :]
            return tuple(carry)
        return lax.fori_loop(0, KLOC // (GRP * 8), body, (zero,) * (2 if last else 1))

    half = KLOC // CH // 2
    fw1 = forward(0)
    own_scores(SPLIT[0], SPLIT[1])
    cslice.wait()
    compact(0, fw1)
    acc = first_pass(0, 0, half, (zero, zero))
    fw2 = forward(1)
    racc, lacc = first_pass(0, half, 2 * half, acc)
    ar1[me, 0:1, :] = rsum(racc)
    ar1[me, 1:2, :] = rsum(lacc)
    x1 = [exchange(0, ar1)]
    compact(1, fw2)
    racc, lacc = first_pass(1, 0, 2 * half, (zero, zero))
    ar1b[me, 0:1, :] = rsum(racc)
    ar1b[me, 1:2, :] = rsum(lacc)
    x1.append(exchange(1, ar1b))

    lse, x2 = [], []
    for v, (b1, b2) in enumerate(((ar1, ar2), (ar1b, ar2b))):
        if v == 1:
            own_scores(SPLIT[1], SPLIT[2])
        tot = total(b1, x1[v])
        lse.append(tot[1:2])
        r, = sweep(v, recip(tot[0:1]), False)
        b2[me] = rsum(r)
        x2.append(exchange(2 + v, b2))

    x3, b_copies = [], []
    eye = (lax.broadcasted_iota(jnp.int32, (128, 128), 0)
           == lax.broadcasted_iota(jnp.int32, (128, 128), 1))
    for v, (b2, b3) in enumerate(((ar2, ar3), (ar2b, ar3b))):
        if v == 1:
            own_scores(SPLIT[2], SPLIT[3])
        tot = total(b2, x2[v])
        r, tl = sweep(v, recip(tot), True)
        b3[me, 0:1, :] = rsum(r)
        b3[me, 1:2, :] = rsum(tl)
        x3.append(exchange(4 + v, b3))
        for t in range(KLOC // 128):
            blk = bcol[v, t * 128:(t + 1) * 128, :]
            b_all[me, v:v + 1, t * 128:(t + 1) * 128] = jnp.sum(
                jnp.where(eye, blk, 0.0), axis=0, keepdims=True)
    for o, peer in enumerate(peers):
        cp = pltpu.make_async_remote_copy(
            src_ref=b_all.at[me], dst_ref=b_all.at[me], send_sem=b_send.at[o],
            recv_sem=b_recv.at[o], device_id=(peer,), device_id_type=MESH)
        cp.start()
        b_copies.append(cp)

    cnt = count[0:1]
    g = 1.0 / (2.0 * SOFT_TEMP * cnt)
    alpha = [m1 * g / x for x in lse]
    stat_ref[1:2, :] = jnp.broadcast_to(g, (1, 128))
    stat_ref[2:3, :] = jnp.broadcast_to(cnt, (1, 128))
    before = jnp.zeros((1, 1), jnp.float32)
    for d in range(NDEV):
        before = before + jnp.where(d < me, 1.0, 0.0) * jnp.sum(mf[d][0:1], axis=1, keepdims=True)
    mine = jnp.broadcast_to(m_all[me].astype(jnp.float32), (8, ROWS))
    pre = dot_nn(mine.astype(jnp.bfloat16), tri)[0:1] + before
    pre = jnp.where(mine[0:1] > 0, pre, -1.0)
    pcol = jnp.sum(jnp.where(eye, jnp.broadcast_to(pre, (128, 128)), 0.0), axis=1, keepdims=True)
    lane = lax.broadcasted_iota(jnp.int32, (128, NS), 1).astype(jnp.float32)
    hit = lane == pcol

    def put(i, x, scale):
        col = jnp.sum(jnp.where(hit, jnp.broadcast_to(x, (128, NS)), 0.0), axis=1, keepdims=True)
        own_ref[i] = jnp.broadcast_to(col, (128, 128))
        y = x * scale
        for t in range(NDEV):
            j = (i + 2) % 4
            vecs_ref[t, j:j + 1, :] = y[:, t * 128:(t + 1) * 128]

    put(2, alpha[0], 1.0)
    put(3, alpha[1], 1.0)
    own_scores(SPLIT[3], NPC)

    tots = [total(ar3, x3[0])]
    a0 = recip(tots[0][0:1])
    put(0, a0, g)
    tots.append(total(ar3b, x3[1]))
    a1 = recip(tots[1][0:1])
    put(1, a1, g)
    inner = sum(a * (tots[v][1:2] * (1.0 / SOFT_TEMP)) - a * tots[v][0:1] * jnp.log(lse[1 - v])
                for v, a in enumerate((a0, a1)))
    loss = -jnp.sum(jnp.where(m1 > 0, inner, 0.0), axis=1, keepdims=True) / (2.0 * cnt)
    stat_ref[0:1, :] = jnp.broadcast_to(loss, (1, 128))

    for cp in b_copies:
        cp.wait_recv()
    for d in range(NDEV):
        lo_col = d * KLOC
        b_out[lo_col // TK, :, lo_col % TK:lo_col % TK + KLOC] = b_all[d]
    for j in range(NPC - NBUF, NPC):
        p_store(j).wait()
    for cp in m_copies + z_copies[0] + z_copies[1] + fw1 + fw2 + sum(x1 + x2 + x3, []) + b_copies:
        cp.wait_send()


def sink_call(z1, z2, m, c):
    f32, bf16 = jnp.float32, jnp.bfloat16
    vm = pl.BlockSpec(memory_space=pltpu.VMEM)
    hbm = pl.BlockSpec(memory_space=pltpu.HBM)
    dma = pltpu.SemaphoreType.DMA
    return pl.pallas_call(
        sink_kernel,
        in_specs=[hbm] * 4,
        out_specs=[vm] * 7 + [hbm],
        out_shape=[
            pltpu.VMEM((NDEV, 2 * ROWS, DIM), bf16),
            pltpu.VMEM((NDEV, 4, ROWS), f32),
            pltpu.VMEM((4, ROWS, 128), f32),
            pltpu.VMEM((KALL // TK, 2, TK), f32),
            pltpu.VMEM((3, 128), f32),
            pltpu.VMEM((2 * ROWS, TK), f32),
            pltpu.VMEM((TK, DIM), bf16),
            jax.ShapeDtypeStruct((2 * ROWS, KALL - TK), f32),
        ],
        scratch_shapes=[
            pltpu.VMEM((2, NDEV, ROWS, DIM), bf16),
            pltpu.VMEM((NDEV, 1, ROWS), jnp.int32),
            pltpu.VMEM((KLOC, DIM), bf16),
            pltpu.VMEM((NS, NS), bf16),
            pltpu.VMEM((2, NS, DIM), bf16),
            pltpu.VMEM((2, KLOC, NS), f32),
            pltpu.VMEM((2, KLOC, NS), f32),
            pltpu.VMEM((2, KLOC, 128), f32),
            pltpu.VMEM((NDEV, 2, NS), f32),
            pltpu.VMEM((NDEV, 2, NS), f32),
            pltpu.VMEM((NDEV, 1, NS), f32),
            pltpu.VMEM((NDEV, 1, NS), f32),
            pltpu.VMEM((NDEV, 2, NS), f32),
            pltpu.VMEM((NDEV, 2, NS), f32),
            pltpu.VMEM((NDEV, 2, KLOC), f32),
            pltpu.VMEM((2 * ROWS, DIM), bf16),
            pltpu.VMEM((NBUF, PCH, DIM), bf16),
            pltpu.VMEM((NBUF, 2 * ROWS, PCH), f32),
            dma(()), dma((5,)),
            dma((7,)), dma((7,)),
            dma((2, 4)), dma((2, 4)),
            dma((2, 3)), dma((2, 3)),
            dma((6, 7)), dma((6, 7)),
            dma((7,)), dma((7,)),
            dma((NBUF,)), dma((NBUF,)),
        ],
        compiler_params=pltpu.CompilerParams(
            collective_id=0, has_side_effects=True, vmem_limit_bytes=VM1 * 1024 * 1024),
        name="sinkhorn",
    )(z1, z2, m, c)


def grad_kernel(c0_ref, c_hbm, w_ref, vecs_ref, own_ref, b_ref, p0_ref, p_hbm, stat_ref,
                q1_hbm, q2_hbm, dz1_ref, dz2_ref, dc_hbm, loss_ref,
                cbuf, pbuf, qbuf, dcbuf, bcol, c_sem, p_sem, q_sem, dc_sem):
    step = pl.program_id(0)
    last = KALL // TK - 1
    slot = lax.rem(step, 2)
    nck = TK // CK

    def p_load(st):
        sl = lax.rem(st, 2)
        return pltpu.make_async_copy(
            p_hbm.at[:, pl.ds(pl.multiple_of((st - 1) * TK, TK), TK)], pbuf.at[sl], p_sem.at[sl])

    def c_load(st):
        sl = lax.rem(st, 2)
        return pltpu.make_async_copy(
            c_hbm.at[pl.ds(pl.multiple_of(st * TK, TK), TK), :], cbuf.at[sl], c_sem.at[sl])

    def q_store(st, v):
        sl = lax.rem(st, 2)
        return pltpu.make_async_copy(
            qbuf.at[sl, v], (q1_hbm, q2_hbm)[v].at[:, pl.ds(pl.multiple_of(st * TK, TK), TK)],
            q_sem.at[sl, v])

    def dc_store(st, k):
        sl = lax.rem(st, 2)
        return pltpu.make_async_copy(
            dcbuf.at[sl, pl.ds(k * CK, CK)],
            dc_hbm.at[pl.ds(pl.multiple_of(st * TK + k * CK, CK), CK), :], dc_sem.at[sl, k])

    @pl.when(step == 0)
    def _():
        dz1_ref[...] = jnp.zeros_like(dz1_ref)
        dz2_ref[...] = jnp.zeros_like(dz2_ref)
        loss_ref[...] = stat_ref[0:1, :]
        pbuf[0] = p0_ref[...]
        cbuf[0] = c0_ref[...]

    @pl.when(step > 0)
    def _():
        p_load(step).wait()
        c_load(step).wait()

    @pl.when(step < last)
    def _():
        p_load(step + 1).start()
        c_load(step + 1).start()

    @pl.when(step >= 2)
    def _():
        for v in range(2):
            q_store(step - 2, v).wait()
        for k in range(nck):
            dc_store(step - 2, k).wait()

    g = stat_ref[1:2, 0:1]
    dz = jnp.zeros((2 * ROWS, DIM), jnp.float32)
    for t in range(TK // OS):
        cols = slice(t * OS, (t + 1) * OS)
        ps = [pbuf[slot, :ROWS, cols], pbuf[slot, ROWS:, cols]]
        qs = []
        for v in range(2):
            arow = jnp.concatenate([own_ref[v]] * (OS // 128), axis=1)
            q = (ps[v] * ps[v] * arow) * b_ref[step, v:v + 1, cols]
            qbuf[slot, v, :, cols] = q
            qs.append(q)
        gs = []
        for v in range(2):
            al = jnp.concatenate([own_ref[2 + v]] * (OS // 128), axis=1)
            gs.append((ps[v] * al - qs[1 - v] * g).astype(jnp.bfloat16))
        dz = dz + dot_nn(jnp.concatenate(gs, axis=0), cbuf[slot, cols, :])
    dz1_ref[...] += dz[:ROWS]
    dz2_ref[...] += dz[ROWS:]

    for v in range(2):
        for t in range(TK // 128):
            blk = jnp.broadcast_to(b_ref[step, v:v + 1, t * 128:(t + 1) * 128], (128, 128))
            bcol[v, t * 128:(t + 1) * 128, :] = jnp.transpose(blk)

    tiles = (jnp.max(stat_ref[2:3, :]).astype(jnp.int32) + (ROWS - 1)) // ROWS

    def piece(t, idx):
        rows = slice(t * SUB, (t + 1) * SUB)
        w = w_ref[idx]
        vec = vecs_ref[idx]
        p = jnp.exp2(dot_nt(cbuf[slot, rows, :], w) * C_EXP)
        p1, p2 = p[:, :ROWS], p[:, ROWS:]
        g1 = p1 * vec[0:1] - (p2 * p2 * bcol[1, rows, :]) * vec[3:4]
        g2 = p2 * vec[1:2] - (p1 * p1 * bcol[0, rows, :]) * vec[2:3]
        gg = jnp.concatenate([g1.astype(jnp.bfloat16), g2.astype(jnp.bfloat16)], axis=1)
        return dot_nn(gg, w)

    npc = TK // SUB

    def add_tiles(idx, n, flush):
        for t in range(npc):
            rows = slice(t * SUB, (t + 1) * SUB)
            dcbuf[slot, rows, :] += sum(piece(t, idx + i) for i in range(n))
            if flush and (t + 1) % (CK // SUB) == 0:
                dc_store(step, t // (CK // SUB)).start()

    for t in range(npc):
        dcbuf[slot, t * SUB:(t + 1) * SUB, :] = piece(t, 0) + piece(t, 1)
    for v in range(2):
        q_store(step, v).start()

    rest = tiles - 2
    fin = jnp.where(rest == 1, 1, jnp.where(rest % 2 == 1, 3, jnp.minimum(rest, 2)))

    def body(i, carry):
        add_tiles(2 + 2 * i, 2, False)
        return carry
    lax.fori_loop(0, (rest - fin) // 2, body, 0)

    for n in (1, 2, 3):
        @pl.when(fin == n)
        def _(n=n):
            add_tiles(tiles - n, n, True)

    @pl.when(fin == 0)
    def _():
        for k in range(nck):
            dc_store(step, k).start()

    @pl.when(step == last)
    def _():
        for st in (last - 1, last):
            for v in range(2):
                q_store(st, v).wait()
            for k in range(nck):
                dc_store(st, k).wait()


def grad_call(c0, c, w, vecs, own, b, p0, p, stat):
    f32, bf16 = jnp.float32, jnp.bfloat16
    whole = lambda shape: pl.BlockSpec(shape, lambda i: (0,) * len(shape))
    hbm = pl.BlockSpec(memory_space=pl.ANY)
    vm = pl.BlockSpec(memory_space=pltpu.VMEM)
    dma = pltpu.SemaphoreType.DMA
    return pl.pallas_call(
        grad_kernel,
        grid=(KALL // TK,),
        in_specs=[
            vm, hbm,
            vm, vm, vm,
            vm,
            vm, hbm,
            vm,
        ],
        out_specs=[hbm, hbm, whole((ROWS, DIM)), whole((ROWS, DIM)), hbm, whole((1, 128))],
        out_shape=[
            jax.ShapeDtypeStruct((ROWS, KALL), f32),
            jax.ShapeDtypeStruct((ROWS, KALL), f32),
            jax.ShapeDtypeStruct((ROWS, DIM), f32),
            jax.ShapeDtypeStruct((ROWS, DIM), f32),
            jax.ShapeDtypeStruct((KALL, DIM), f32),
            jax.ShapeDtypeStruct((1, 128), f32),
        ],
        scratch_shapes=[
            pltpu.VMEM((2, TK, DIM), bf16),
            pltpu.VMEM((2, 2 * ROWS, TK), f32),
            pltpu.VMEM((2, 2, ROWS, TK), f32),
            pltpu.VMEM((2, TK, DIM), f32),
            pltpu.VMEM((2, TK, 128), f32),
            dma((2,)), dma((2,)), dma((2, 2)), dma((2, TK // CK)),
        ],
        compiler_params=pltpu.CompilerParams(vmem_limit_bytes=VM2 * 1024 * 1024),
        name="grads",
    )(c0, c, w, vecs, own, b, p0, p, stat)


def solution(mesh):
    def local_step(view_one, view_two, protos, valid_mask):
        w, vecs, own, b, stat, p0, c0, p = sink_call(
            view_one, view_two, valid_mask.reshape(1, ROWS), protos)
        q1, q2, dz1, dz2, dc, loss = grad_call(
            c0, protos, w, vecs, own, b, p0, p, stat)
        return q1, q2, loss[0, 0], dz1, dz2, dc

    return jax.shard_map(
        local_step,
        mesh=mesh,
        in_specs=(P("data", None), P("data", None), P(None, None), P("data")),
        out_specs=(P("data", None), P("data", None), P(), P("data", None), P("data", None), P(None, None)),
        check_vma=False,
    )
```

profile of v0, /device:TPU:0, one launch (start us, length us, event | category | flops | bytes accessed | tf_op | source)
XLA Modules:
  0.0 60.7 jit_solution(13036121500820752980)
XLA Ops:
  0.6 32.2 %sinkhorn.1 = (bf16[8,256,256]{2,1,0:T(8,128)(2,1)S(1)}, f32[8,4,128]{2,1,0:T(4,128)S(1)}, f32[4,128,128]{2,1,0:T(8,128)S(1)}, f32[4,2,4096]{2,1,0:T(2,128)S(1)}...) custom-call(bf16[128,256]{1,0:T(8,128)(2,1)} %z1_hbm.1, ...), custom_call_target="tpu_custom_call" | custom-call | tf_op jit(solution)/shard_map/sinkhorn/pallas_call | solution.py:341
  32.9 27.6 %grads.1 = (f32[128,16384]{1,0:T(8,128)}, f32[128,16384]{1,0:T(8,128)}, f32[128,256]{1,0:T(8,128)}, f32[128,256]{1,0:T(8,128)}, f32[16384,256]{1,0:T(8,128)}, /*index=5*/f32[1,128]{1,0:T(1,128)}) custom-call(bf16[4096,256]{1,0:T(8,128)(2,1)S(1)} %get-tuple-element.20.c0_ref, bf16[16384,256]{1,0:T(8,128)(2,1)} %c_hbm.3, ...), custom_call_target="tpu_custom_call" | custom-call | tf_op jit(solution)/shard_map/grads/pallas_call | solution.py:527
where the time goes:
time: 60.8 us; the launch traced here: 60.7 us
  Pallas kernels  59.9 us (99%)
  between operations  0.8 us (1%)
    pallas_call x1, Pallas kernels, sink_call(): pl.pallas_call(sink_kernel, in_specs=[hbm] * 4, out_specs=[vm] * 7 + [hbm...  32.2 us
    pallas_call x1, Pallas kernels, grad_call(): pl.pallas_call(grad_kernel, grid=(KALL // TK,), in_specs=[vm, hbm, vm, vm...  27.6 us

commit v1 on v0

--- a/solution.py
+++ b/solution.py
@@ -18,7 +18,7 @@
 KALL = 16384
 KLOC = KALL // NDEV
 GRP = 128
-CH = 256
+CH = 512
 TK = 4096
 SUB = 512
 CK = 1024

time: 60.8 us -> 65.4 us (1.076)
  Pallas kernels: 59.9 us -> 64.4 us
    pallas_call x1, Pallas kernels: 27.6 us -> 32.3 us  [grad_call(): pl.pallas_call(grad_kernel, grid=(KALL // TK,), in_specs=[vm, hbm, vm, vm...]
where the time goes in v1:
time: 65.4 us; the launch traced here: 65.2 us
  Pallas kernels  64.4 us (98%)
  between operations  0.8 us (1%)
    pallas_call x1, Pallas kernels, grad_call(): pl.pallas_call(grad_kernel, grid=(KALL // TK,), in_specs=[vm, hbm, vm, vm...  32.3 us
    pallas_call x1, Pallas kernels, sink_call(): pl.pallas_call(sink_kernel, in_specs=[hbm] * 4, out_specs=[vm] * 7 + [hbm...  32.1 us

profile of v1, /device:TPU:0, one launch (start us, length us, event | category | flops | bytes accessed | tf_op | source)
XLA Modules:
  0.0 65.2 jit_solution(9488228127155469493)
XLA Ops:
  0.6 32.1 %sinkhorn.1 = (bf16[8,256,256]{2,1,0:T(8,128)(2,1)S(1)}, f32[8,4,128]{2,1,0:T(4,128)S(1)}, f32[4,128,128]{2,1,0:T(8,128)S(1)}, f32[4,2,4096]{2,1,0:T(2,128)S(1)}...) custom-call(bf16[128,256]{1,0:T(8,128)(2,1)} %z1_hbm.1, ...), custom_call_target="tpu_custom_call" | custom-call | tf_op jit(solution)/shard_map/sinkhorn/pallas_call | solution.py:341
  32.7 32.3 %grads.1 = (f32[128,16384]{1,0:T(8,128)}, f32[128,16384]{1,0:T(8,128)}, f32[128,256]{1,0:T(8,128)}, f32[128,256]{1,0:T(8,128)}, f32[16384,256]{1,0:T(8,128)}, /*index=5*/f32[1,128]{1,0:T(1,128)}) custom-call(bf16[4096,256]{1,0:T(8,128)(2,1)S(1)} %get-tuple-element.20.c0_ref, bf16[16384,256]{1,0:T(8,128)(2,1)} %c_hbm.3, ...), custom_call_target="tpu_custom_call" | custom-call | tf_op jit(solution)/shard_map/grads/pallas_call | solution.py:527
